TPU v7x, 32 devices: a whole 2x2x4 slice. The times are simulated.
32 devices in a mesh: group: 8 (over z, y), local: 4 (over x, core).
Axes of the slice: x: 2, y: 2, z: 4, core: 2. Of those that a mesh axis runs over, the one named last changes fastest.
Arguments:
- dense_vec: bfloat16 [4096, 128], P(('group', 'local')), may hold values from -6 to 6
- q_tables: float32 [1024, 26, 128], P('group'), may hold values from -4 to 4
- r_tables: float32 [256, 26, 128], P('local'), may hold values from -4 to 4
- owner: int32 [4096, 26, 1], P(('group', 'local')), may hold values from 0 to 7; in each aligned block of 3328 rows (0 to 3327, 3328 to 6655, ..., all dimensions but the last counted through in order) at most 832 rows name the same one
- q_local: int32 [4096, 26], P(('group', 'local')), may hold values from 0 to 127
- r_index: int32 [4096, 26], P(('group', 'local')), may hold values from 0 to 255
- w_one: bfloat16 [479, 1024], replicated, may hold values from -0.25 to 0.25
- b_one: float32 [1024], replicated, may hold values from -3 to 3
- w_two: bfloat16 [1024, 1024], replicated, may hold values from -0.1875 to 0.1875
- b_two: float32 [1024], replicated, may hold values from -3 to 3
- w_three: bfloat16 [1024, 512], replicated, may hold values from -0.1875 to 0.1875
- b_three: float32 [512], replicated, may hold values from -3 to 3
- w_four: bfloat16 [512, 256], replicated, may hold values from -0.25 to 0.25
- b_four: float32 [256], replicated, may hold values from -3 to 3
- cotangent: bfloat16 [4096, 256], P(('group', 'local')), may hold values from -6 to 6
Outputs:
- q_new: float32 [1024, 26, 128], P('group')
- r_new: float32 [256, 26, 128], P('local')
- w_one_new: float32 [479, 1024], replicated
- b_one_new: float32 [1024], replicated
- w_two_new: float32 [1024, 1024], replicated
- b_two_new: float32 [1024], replicated
- w_three_new: float32 [1024, 512], replicated
- b_three_new: float32 [512], replicated
- w_four_new: float32 [512, 256], replicated
- b_four_new: float32 [256], replicated
Inputs may be any that keep to these rules, and one draw needn't show every extreme that they name: `owner`: within the rows of one device (its 128 samples times 26 tables), no group is named more than 832 times, a bound that some block reaches.
All inputs are finite; a program needn't handle non-finite values.
Results may differ from a plain program's by a relative error of at most 0.0025.
Values may be sent and summed in bfloat16 or wider, within the bound.
A program may use at most 128 MiB of HBM per device.

v0:
```python
import jax
import jax.numpy as jnp
import numpy as np
from jax import lax
from jax.sharding import PartitionSpec as P

table_rate = 0.05
dense_rate = 0.0005


def silu_slope(preact):
    sigma = jax.nn.sigmoid(preact)
    return sigma * (1.0 + preact * (1.0 - sigma))


def interact(dense_rows, embeds):
    vectors_all = jnp.concatenate([dense_rows[:, None, :], embeds], axis=1).astype(jnp.float32)
    gram_mat = jnp.einsum("bid,bjd->bij", vectors_all, vectors_all, precision=lax.Precision.HIGHEST)
    lower_i, lower_j = np.tril_indices(vectors_all.shape[1], -1)
    pair_vals = gram_mat[:, lower_i, lower_j]
    features = jnp.concatenate([dense_rows.astype(jnp.float32), pair_vals], axis=1).astype(
        jnp.bfloat16
    )
    return (vectors_all, features)


def pair_back(d_pairs, vectors_all):
    vectors = vectors_all.shape[1]
    lower_i, lower_j = np.tril_indices(vectors, -1)
    spread = (
        jnp.zeros((vectors_all.shape[0], vectors, vectors), jnp.float32)
        .at[:, lower_i, lower_j]
        .set(d_pairs)
    )
    spread = spread + jnp.swapaxes(spread, 1, 2)
    return jnp.einsum("bij,bjd->bid", spread, vectors_all, precision=lax.Precision.HIGHEST)


def contract_rows(left, right):
    return lax.dot_general(
        left, right, (((0,), (0,)), ((), ())), preferred_element_type=jnp.float32
    )


def dense_pass(features, layers, cot_rows):
    inputs_list = [features]
    pre_list = []
    current = features
    for layer_idx, (weight, biases) in enumerate(layers):
        pre_act = jnp.dot(current, weight, preferred_element_type=jnp.float32) + biases
        pre_list.append(pre_act)
        if layer_idx + 1 < len(layers):
            current = jax.nn.silu(pre_act).astype(jnp.bfloat16)
            inputs_list.append(current)
    grad_low = cot_rows
    grad_full = cot_rows.astype(jnp.float32)
    grads = []
    back_grad = None
    for layer_idx in reversed(range(len(layers))):
        weight = layers[layer_idx][0]
        w_grad = contract_rows(inputs_list[layer_idx], grad_low)
        b_grad = jnp.sum(grad_full, axis=0)
        back_grad = lax.dot_general(
            grad_low, weight, (((1,), (1,)), ((), ())), preferred_element_type=jnp.float32
        )
        grads.insert(0, (w_grad, b_grad))
        if layer_idx > 0:
            grad_full = back_grad * silu_slope(pre_list[layer_idx - 1])
            grad_low = grad_full.astype(jnp.bfloat16)
    return (grads, back_grad)


def body(
    dense_vec,
    q_tables,
    r_tables,
    owner,
    q_local,
    r_index,
    w_one,
    b_one,
    w_two,
    b_two,
    w_three,
    b_three,
    w_four,
    b_four,
    cotangent,
):
    layers = [(w_one, b_one), (w_two, b_two), (w_three, b_three), (w_four, b_four)]
    groups = lax.axis_size("group")
    batch_rows, table_count = q_local.shape
    embed_width = q_tables.shape[2]
    lookups = batch_rows * table_count
    capacity = 2 * lookups // groups
    slot_count = groups * capacity
    segment_count = q_tables.shape[0] * table_count
    table_ids = jnp.arange(table_count, dtype=jnp.int32)[None, :]
    highest = lax.Precision.HIGHEST
    dest_group = owner[:, :, 0]
    owner_hits = (
        dest_group[:, :, None] == jnp.arange(groups, dtype=jnp.int32)[None, None, :]
    ).astype(jnp.float32)
    table_lower = (jnp.arange(table_count)[:, None] < jnp.arange(table_count)[None, :]).astype(
        jnp.float32
    )
    sample_lower = (jnp.arange(batch_rows)[:, None] < jnp.arange(batch_rows)[None, :]).astype(
        jnp.float32
    )
    within = jnp.einsum("st,bsg->btg", table_lower, owner_hits, precision=highest)
    before = jnp.einsum("cb,cg->bg", sample_lower, jnp.sum(owner_hits, axis=1), precision=highest)
    slot_rank = jnp.sum((within + before[:, None, :]) * owner_hits, axis=2).astype(jnp.int32)
    position = (dest_group * capacity + slot_rank).reshape(lookups)
    source = (
        jnp.full((slot_count,), lookups, jnp.int32)
        .at[position]
        .set(jnp.arange(lookups, dtype=jnp.int32))
    )
    row_keys = (q_local * table_count + table_ids).reshape(lookups)
    keys_padded = jnp.concatenate([row_keys, jnp.zeros((1,), jnp.int32)])
    outgoing = keys_padded[source].reshape(groups, capacity)
    flat_table = q_tables.reshape(segment_count, embed_width)
    request = lax.all_to_all(outgoing, "group", split_axis=0, concat_axis=0, tiled=True)
    served_rows = flat_table[request].astype(jnp.bfloat16)
    arrived = lax.all_to_all(served_rows, "group", split_axis=0, concat_axis=0, tiled=True)
    q_rows = arrived.reshape(slot_count, embed_width)[position]
    full_r = lax.all_gather(r_tables, "local", axis=0, tiled=True)
    remainder_count = full_r.shape[0]
    r_pick = (
        r_index[:, :, None] == jnp.arange(remainder_count, dtype=jnp.int32)[None, None, :]
    ).astype(jnp.float32)
    r_rows = jnp.einsum("btr,rtd->btd", r_pick, full_r, precision=highest).reshape(
        lookups, embed_width
    )
    q_val = q_rows.astype(jnp.float32)
    embeds = (q_val * r_rows).astype(jnp.bfloat16).reshape(batch_rows, table_count, embed_width)
    vectors_all, features = interact(dense_vec, embeds)
    grads, d_features = dense_pass(features, layers, cotangent)
    d_embed = pair_back(d_features[:, embed_width:], vectors_all)[:, 1:, :].reshape(
        lookups, embed_width
    )
    grad_padded = jnp.concatenate(
        [d_embed * r_rows, jnp.zeros((1, embed_width), jnp.float32)], axis=0
    )
    outbound = grad_padded[source].reshape(groups, capacity, embed_width)
    returned = (
        lax.all_to_all(
            outbound.astype(jnp.bfloat16), "group", split_axis=0, concat_axis=0, tiled=True
        )
        .astype(outbound.dtype)
        .reshape(slot_count, embed_width)
    )
    served_flat = request.reshape(slot_count)
    q_part = jax.ops.segment_sum(returned, served_flat, num_segments=segment_count).reshape(
        q_tables.shape
    )
    q_piece = lax.psum_scatter(
        q_part.astype(jnp.bfloat16), "local", scatter_dimension=0, tiled=True
    ).astype(jnp.float32)
    quarter = q_piece.shape[0]
    own_rows = lax.dynamic_slice_in_dim(q_tables, lax.axis_index("local") * quarter, quarter, 0)
    q_new = lax.all_gather(own_rows - table_rate * q_piece, "local", axis=0, tiled=True)
    r_part = jnp.einsum(
        "btr,btd->rtd",
        r_pick,
        (d_embed * q_val).reshape(batch_rows, table_count, embed_width),
        precision=highest,
    )
    summed = lax.psum(r_part, ("group", "local"))
    r_grad = lax.dynamic_slice_in_dim(
        summed, lax.axis_index("local") * r_tables.shape[0], r_tables.shape[0], 0
    )
    r_new = r_tables - table_rate * r_grad
    grad_wa, grad_ba, grad_wb, grad_bb, grad_wc, grad_bc, grad_wd, grad_bd = lax.psum(
        (
            grads[0][0],
            grads[0][1],
            grads[1][0],
            grads[1][1],
            grads[2][0],
            grads[2][1],
            grads[3][0],
            grads[3][1],
        ),
        ("group", "local"),
    )
    summed_grads = [(grad_wa, grad_ba), (grad_wb, grad_bb), (grad_wc, grad_bc), (grad_wd, grad_bd)]
    updated = []
    for (weight, biases), (w_grad, b_grad) in zip(layers, summed_grads):
        updated.append(weight.astype(jnp.float32) - dense_rate * w_grad)
        updated.append(biases - dense_rate * b_grad)
    return (
        q_new,
        r_new,
        updated[0],
        updated[1],
        updated[2],
        updated[3],
        updated[4],
        updated[5],
        updated[6],
        updated[7],
    )


def solution(mesh):
    return jax.shard_map(
        body,
        mesh=mesh,
        in_specs=(
            P(("group", "local"), None),
            P("group", None, None),
            P("local", None, None),
            P(("group", "local"), None, None),
            P(("group", "local"), None),
            P(("group", "local"), None),
            P(),
            P(),
            P(),
            P(),
            P(),
            P(),
            P(),
            P(),
            P(("group", "local"), None),
        ),
        out_specs=(
            P("group", None, None),
            P("local", None, None),
            P(),
            P(),
            P(),
            P(),
            P(),
            P(),
            P(),
            P(),
        ),
        check_vma=False,
    )
```

profile of v0, /device:TPU:0, one launch (start us, length us, event | category | flops | bytes accessed | tf_op | source)
XLA Modules:
  0.0 590.5 jit_solution(14401636984354006459)
XLA Ops:
  11.3 12.8 %scatter_custom_fusion = s32[6656]{0:T(1024)S(1)} fusion(s32[3328]{0:T(1024)S(1)} %fusion.38, s32[3328]{0:T(1024)S(1)} %iota.29, s32[]{:T(128)} %constant.27.clone.1), kind=kCustom, calls=%fused_computation.84 | custom fusion | bytes 26628 | tf_op jit(solution)/shard_map/scatter | solution.py:117
  24.1 34.5 %gather_fusion = s32[6656]{0:T(1024)S(1)} fusion(s32[3329]{0:T(1024)S(1)} %pad_add_fusion, s32[7168]{0:T(1024)S(1)} %pad_clamp_fusion.1), kind=kCustom, calls=%fused_computation | custom fusion | bytes 79872 | tf_op jit(solution)/shard_map/gather | solution.py:121
  59.4 7.3 %all-to-all-start = ((s32[8,1,832]{2,1,0:T(1,128)}), s32[8,1,832]{2,1,0:T(1,128)S(1)}, u32[]{:S(2)}, u32[]{:S(2)}) async-start(s32[8,1,832]{2,1,0:T(1,128)} %all_to_all.14), calls=%async_computation | async-start | bytes 57344 | tf_op jit(solution)/shard_map/all_to_all | solution.py:123
  66.7 2.5 copy.64
  69.4 4.0 all-to-all-done
  73.5 14.3 %gather_fusion.1 = bf16[6656,128]{1,0:T(8,128)(2,1)} fusion(bf16[3328,128]{1,0:T(8,128)(2,1)S(1)} %reshape.127, s32[7168]{0:T(1024)S(1)} %pad_clamp_fusion), kind=kCustom, calls=%fused_computation.1 | custom fusion | bytes 3434496 | tf_op jit(solution)/shard_map/gather | solution.py:124
  87.8 3.8 all-to-all-start.1
  91.7 38.3 %all-to-all-done.1 = bf16[8,832,128]{2,1,0:T(8,128)(2,1)S(1)} async-done(((bf16[8,832,128]{2,1,0:T(8,128)(2,1)}), bf16[8,832,128]{2,1,0:T(8,128)(2,1)S(1)}, u32[]{:S(2)}, u32[]{:S(2)}) %all-to-all-start.1) | async-done | bytes 1703968 | tf_op jit(solution)/shard_map/all_to_all | solution.py:125
  130.0 6.5 %gather_fusion.2 = bf16[3328,128]{1,0:T(8,128)(2,1)S(1)} fusion(bf16[6656,128]{1,0:T(8,128)(2,1)S(1)} %bitcast.53, s32[4096]{0:T(1024)S(1)} %pad_clamp_fusion.2), kind=kCustom, calls=%fused_computation.2 | custom fusion | bytes 1717248 | tf_op jit(solution)/shard_map/gather | solution.py:126
  137.2 7.3 %fusion.5 = (bf16[128,26,128]{2,0,1:T(8,128)(2,1)S(1)}, f32[26,128,128]{2,1,0:T(8,128)}) fusion(f32[128,26,128]{2,1,0:T(8,128)S(1)} %reshape.131, f32[256,26,128]{2,0,1:T(8,128)} %all-gather.3.cloned.1.call-done, s32[128,26]{0,1:T(8,128)S(1)} %copy-done.28), kind=kOutput, calls=%fused_computation.19 | convolution fusion | flops 1310326784 | bytes 7681024 | tf_op jit(solution)/shard_map/btr,rtd->btd/dot_general | solution.py:132
  146.4 4.9 gather_fusion.3
  152.9 2.3 convolution_add_fusion.1
  160.7 19.0 %scatter_fusion = f32[128,27,27]{0,2,1:T(8,128)S(1)} fusion(f32[128,27,27]{0,2,1:T(8,128)S(1)} %broadcast_in_dim.21, s32[351]{0:T(512)S(1)} %copy-done, f32[351,128]{1,0:T(8,128)S(1)} %convolution_bitcast_fusion), kind=kCustom, calls=%fused_computation.6 | custom fusion | bytes 541944 | tf_op jit(solution)/shard_map/scatter | solution.py:33
  180.0 2.9 copy.87
  182.9 3.3 fusion.14
  190.2 15.5 %gather_fusion.4 = bf16[6656,128]{1,0:T(8,128)(2,1)} fusion(bf16[3329,128]{1,0:T(8,128)(2,1)S(1)} %concatenate.24, s32[7168]{0:T(1024)} %copy-done.22), kind=kCustom, calls=%fused_computation.4 | custom fusion | bytes 3434496 | tf_op jit(solution)/shard_map/gather | solution.py:145
  205.7 4.4 all-to-all-start.2
  210.3 39.2 %all-to-all-done.2 = bf16[8,832,128]{2,1,0:T(8,128)(2,1)} async-done(((bf16[8,832,128]{2,1,0:T(8,128)(2,1)}), bf16[8,832,128]{2,1,0:T(8,128)(2,1)}, u32[]{:S(2)}, u32[]{:S(2)}) %all-to-all-start.2) | async-done | bytes 1703968 | tf_op jit(solution)/shard_map/all_to_all | solution.py:147
  249.5 40.3 %scatter_custom_fusion.2 = f32[3328,128]{1,0:T(8,128)} fusion(s32[6656]{0:T(1024)S(1)} %reshape.188, bf16[6656,128]{1,0:T(8,128)(2,1)} %bitcast.13, f32[]{:T(128)} %constant.24.clone.1), kind=kCustom, calls=%fused_computation.9 | custom fusion | flops 1703936 | bytes 3407876 | tf_op jit(solution)/shard_map/scatter-add | solution.py:154
  292.7 2.1 fusion.20
  296.5 1.8 fusion.28
  298.3 2.8 fusion.24
  301.1 6.2 %fusion.4 = f32[256,26,128]{0,2,1:T(8,128)} fusion(s32[128,26]{0,1:T(8,128)S(1)} %copy-done.28, f32[128,26,128]{2,1,0:T(8,128)S(1)} %fusion.14, f32[128,26,128]{2,1,0:T(8,128)S(1)} %copy-done.2), kind=kOutput, calls=%fused_computation.16 | convolution fusion | flops 1309900800 | bytes 6829056 | tf_op jit(solution)/shard_map/btr,btd->rtd/dot_general | solution.py:163
  307.3 14.6 %reduce-scatter.2.cloned.1.call-done = bf16[32,26,128]{2,1,0:T(8,128)(2,1)} async-done(((bf16[128,26,128]{2,1,0:T(8,128)(2,1)}), bf16[32,26,128]{2,1,0:T(8,128)(2,1)}) %reduce-scatter.2.cloned.1.call-update) | async-done | bytes 213008 | tf_op jit(solution)/shard_map/reduce_scatter | solution.py:157
  324.8 40.8 %all-reduce.1 = (f32[1024]{0:T(1024)S(1)}, f32[1024]{0:T(1024)S(1)}, f32[512]{0:T(512)S(1)}, f32[256]{0:T(256)S(1)}) all-reduce(f32[1024]{0:T(1024)S(1)} %copy-done.34, f32[1024]{0:T(1024)S(1)} %copy-done.33, f32[512]{0:T(512)S(1)} %copy-done.37, f32[256]{0:T(256)S(1)} %convert_reduce_fusion), channel_id=1, replica_groups=mesh['group'=8,'local'=4] {'group','local'}, use_global_device_ids=true, to_apply=%region_9.10 | all-reduce | flops 2816 | bytes 22528 | tf_op jit(solution)/shard_map/psum | solution.py:174
  367.4 192.2 %all-reduce.5.cloned.1.call-done = (f32[256,26,128]{0,2,1:T(8,128)}, f32[479,1024]{1,0:T(8,128)}, f32[1024,1024]{1,0:T(8,128)}, f32[1024,512]{1,0:T(8,128)}, f32[512,256]{1,0:T(8,128)}) async-done(((f32[256,26,128]{0,2,1:T(8,128)}, f32[479,1024]{1,0:T(8,128)}, f32[1024,1024]{1,0:T(8,128)}, f32[1024,512]{1,0:T(8,128)}, f32[512,256]{1,0:T(8,128)}), (f32[256,26,128]{0,2,1:T(8,128)}, f32[479,1024]{1,0:T(8,128)}, ...) | async-done | bytes 12185616 | tf_op jit(solution)/shard_map/psum | solution.py:169
  559.5 2.0 multiply_subtract_fusion.3
  562.9 1.9 multiply_subtract_fusion.4
  564.8 3.4 multiply_subtract_fusion.2
  571.3 2.7 multiply_subtract_fusion
  574.0 7.2 %all-gather.5.cloned.1.call-done = f32[128,26,128]{2,0,1:T(8,128)} async-done(((f32[32,26,128]{2,0,1:T(8,128)}), f32[128,26,128]{2,0,1:T(8,128)}) %all-gather.5.cloned.1.call-update) | async-done | bytes 1703952 | tf_op jit(solution)/shard_map/all_gather | solution.py:162
  581.2 2.8 copy.112
  (145 shorter events, 32.8 us)
Async XLA Ops:
  7.2 129.6 %all-gather.3.cloned.1.call-start = ((), (), s32[]{:S(2)}) async-start(), calls=%async_computation.4 | async-start | bytes 4259840 | tf_op jit(solution)/shard_map/all_gather | solution.py:127
  24.1 34.6 %copy-start.22 = (s32[7168]{0:T(1024)}, s32[7168]{0:T(1024)S(1)}, u32[]{:S(2)}) copy-start(s32[7168]{0:T(1024)S(1)} %pad_clamp_fusion.1) | copy-start | bytes 86020
  59.4 14.0 %all-to-all-start = ((s32[8,1,832]{2,1,0:T(1,128)}), s32[8,1,832]{2,1,0:T(1,128)S(1)}, u32[]{:S(2)}, u32[]{:S(2)}) async-start(s32[8,1,832]{2,1,0:T(1,128)} %all_to_all.14), calls=%async_computation | async-start | bytes 57344 | tf_op jit(solution)/shard_map/all_to_all | solution.py:123
  69.1 18.6 %copy-start.3 = (f32[128,26,128]{2,1,0:T(8,128)}, f32[128,26,128]{2,1,0:T(8,128)S(1)}, u32[]{:S(2)}) copy-start(f32[128,26,128]{2,1,0:T(8,128)S(1)} %copy.64) | copy-start | bytes 5111812
  73.3 14.4 %copy-start.23 = (s32[8,1,832]{2,1,0:T(1,128)}, s32[8,1,832]{2,1,0:T(1,128)S(1)}, u32[]{:S(2)}) copy-start(s32[8,1,832]{2,1,0:T(1,128)S(1)} %all-to-all-done) | copy-start | bytes 79876
  87.8 3.8 copy-start.25
  87.8 42.2 %all-to-all-start.1 = ((bf16[8,832,128]{2,1,0:T(8,128)(2,1)}), bf16[8,832,128]{2,1,0:T(8,128)(2,1)S(1)}, u32[]{:S(2)}, u32[]{:S(2)}) async-start(bf16[8,832,128]{2,1,0:T(8,128)(2,1)} %bitcast.55), calls=%async_computation.1 | async-start | bytes 3407872 | tf_op jit(solution)/shard_map/all_to_all | solution.py:125
  136.7 7.8 %copy-start.1 = (f32[128,26,128]{2,1,0:T(8,128)}, f32[128,26,128]{2,1,0:T(8,128)S(1)}, u32[]{:S(2)}) copy-start(f32[128,26,128]{2,1,0:T(8,128)S(1)} %reshape.131) | copy-start | bytes 5111812
  144.6 6.7 %copy-start.31 = (f32[1024]{0:T(1024)S(1)}, f32[1024]{0:T(1024)}, u32[]{:S(2)}) copy-start(f32[1024]{0:T(1024)} %param.30) | copy-start | bytes 12292
  145.3 7.6 %copy-start.32 = (f32[1024]{0:T(1024)S(1)}, f32[1024]{0:T(1024)}, u32[]{:S(2)}) copy-start(f32[1024]{0:T(1024)} %param.32) | copy-start | bytes 12292
  152.8 5.4 copy-start.11
  152.8 2.3 copy-start.14
  157.1 3.1 copy-start.26
  160.3 19.4 %copy-start.20 = (bf16[128,1024]{1,0:T(8,128)(2,1)}, bf16[128,1024]{1,0:T(8,128)(2,1)S(1)}, u32[]{:S(2)}) copy-start(bf16[128,1024]{1,0:T(8,128)(2,1)S(1)} %get-tuple-element.52) | copy-start | bytes 786436
  182.9 3.3 copy-start.4
  205.7 4.5 copy-start.24
  205.7 43.8 %all-to-all-start.2 = ((bf16[8,832,128]{2,1,0:T(8,128)(2,1)}), bf16[8,832,128]{2,1,0:T(8,128)(2,1)}, u32[]{:S(2)}, u32[]{:S(2)}) async-start(bf16[8,832,128]{2,1,0:T(8,128)(2,1)} %bitcast.54), calls=%async_computation.2 | async-start | bytes 3407872 | tf_op jit(solution)/shard_map/all_to_all | solution.py:147
  210.1 111.8 %reduce-scatter.2.cloned.1.call-start = ((), (), s32[]{:S(2)}) async-start(), calls=%async_computation.5 | async-start | bytes 1310720 | tf_op jit(solution)/shard_map/reduce_scatter | solution.py:157
  292.6 3.9 copy-start.18
  292.6 3.9 copy-start.27
  292.6 266.9 %all-reduce.5.cloned.1.call-start = ((), (), s32[]{:S(2)}) async-start(), calls=%async_computation.7 | async-start | bytes 24379392 | tf_op jit(solution)/shard_map/psum | solution.py:169
  294.8 3.5 copy-start.12
  298.3 2.8 copy-start.2
  307.3 16.9 %copy-start.8 = (f32[64,26,128]{2,0,1:T(8,128)S(1)}, f32[64,26,128]{2,0,1:T(8,128)}, u32[]{:S(2)}) copy-start(f32[64,26,128]{2,0,1:T(8,128)} %param.25) | copy-start | bytes 2555908
  307.3 273.9 %all-gather.5.cloned.1.call-start = ((), (), s32[]{:S(2)}) async-start(), calls=%async_computation.6 | async-start | bytes 2129920 | tf_op jit(solution)/shard_map/all_gather | solution.py:162
  323.1 42.5 %copy-start.38 = (f32[256]{0:T(256)S(1)}, f32[256]{0:T(256)}, u32[]{:S(2)}) copy-start(f32[256]{0:T(256)} %param.36) | copy-start | bytes 3076
  323.2 43.0 %copy-start.36 = (f32[512]{0:T(512)S(1)}, f32[512]{0:T(512)}, u32[]{:S(2)}) copy-start(f32[512]{0:T(512)} %param.34) | copy-start | bytes 6148
  561.5 3.3 copy-start.7
  562.9 5.3 copy-start.15
  564.8 3.4 copy-start.13
  564.8 5.1 copy-start.10
  568.2 3.0 copy-start.5
  (15 other events, 24.0 us)
Sparse Core Ops, SparseCore 0:
  9.5 32.7 all-gather.2
  292.7 29.1 reduce-scatter.1
  328.9 230.5 all-reduce.4
  561.5 19.5 all-gather.4
where the time goes:
time: 592 us; the launch traced here: 591 us
  waiting for transfers between devices  296 us (50%)
  local copies, waits for them, and re-layouts  130 us (22%)
  other arithmetic  59.6 us (10%)
  blocking collectives  40.8 us (7%)
  matrix products  34 us (6%)
  starting transfers between devices  15.7 us (3%)
  between operations  14.4 us (2%)
    psum x1, waiting for transfers between devices, body(): summed = lax.psum(r_part, ('group', 'local'))  192 us
    psum x1, blocking collectives, body(): lax.psum((grads[0][0], grads[0][1], grads[1][0], grads[1][1], grads[2][0]...  40.8 us
    scatter-add x1, other arithmetic, body(): jax.ops.segment_sum(returned, served_flat, num_segments=segment_count)  40.3 us
    all_to_all x1, waiting for transfers between devices, body(): lax.all_to_all(outbound.astype(jnp.bfloat16), 'group', split_axis=0, conc...  39.2 us
    all_to_all x1, waiting for transfers between devices, body(): lax.all_to_all(served_rows, 'group', split_axis=0, concat_axis=0, tiled=T...  38.3 us
    gather x1, local copies, waits for them, and re-layouts, body(): outgoing = keys_padded[source].reshape(groups, capacity)  34.5 us
    scatter x1, local copies, waits for them, and re-layouts, pair_back(): spread = jnp.zeros((vectors_all.shape[0], vectors, vectors), jnp.float32)...  19 us
    gather x1, local copies, waits for them, and re-layouts, body(): outbound = grad_padded[source].reshape(groups, capacity, embed_width)  15.5 us
  transfers between devices with their start and end apart: 7, of which 6 were waited for; matrix products, arithmetic and copies ran while one was open for 18% of the time, Pallas kernels for 0%

commit v1 on v0

--- a/solution.py
+++ b/solution.py
@@ -166,7 +166,8 @@
         (d_embed * q_val).reshape(batch_rows, table_count, embed_width),
         precision=highest,
     )
-    summed = lax.psum(r_part, ("group", "local"))
+    inner = lax.psum(r_part, "group")
+    summed = lax.psum(inner, "local")
     r_grad = lax.dynamic_slice_in_dim(
         summed, lax.axis_index("local") * r_tables.shape[0], r_tables.shape[0], 0
     )

time: 592 us -> 681 us (1.15)
  waiting for transfers between devices: 296 us -> 389 us
    psum x1 -> x3, waiting for transfers between devices: 192 us -> 241 us  [the longest x1 144 us: body(): lax.psum((grads[0][0], grads[0][1], grads[1][0], grads[1][1], grads[2][0]...]
    all_to_all x1, waiting for transfers between devices: 39.2 us -> 58.9 us  [body(): lax.all_to_all(outbound.astype(jnp.bfloat16), 'group', split_axis=0, conc...]
    reduce_scatter x1, waiting for transfers between devices: 14.6 us -> 26.9 us  [body(): lax.psum_scatter(q_part.astype(jnp.bfloat16), 'local', scatter_dimension=...]
    all_gather x1, waiting for transfers between devices: 7.17 us -> 19.2 us  [body(): lax.all_gather(own_rows - table_rate * q_piece, 'local', axis=0, tiled=True)]
    unnamed x87 -> x73, local copies, waits for them, and re-layouts: 14.2 us -> 15.2 us
  transfers between devices with their start and end apart: 7 -> 9, of which waited for: 6 -> 8; matrix products, arithmetic and copies ran while one was open for 18% -> 24% of each run, Pallas kernels for 0% -> 0%
where the time goes in v1:
time: 681 us; the launch traced here: 680 us
  waiting for transfers between devices  389 us (57%)
  local copies, waits for them, and re-layouts  128 us (19%)
  other arithmetic  60.9 us (9%)
  blocking collectives  41.1 us (6%)
  matrix products  30.6 us (4%)
  starting transfers between devices  15.3 us (2%)
  between operations  14.8 us (2%)
    psum x1, waiting for transfers between devices, body(): lax.psum((grads[0][0], grads[0][1], grads[1][0], grads[1][1], grads[2][0]...  144 us
    psum x1, waiting for transfers between devices, body(): summed = lax.psum(inner, 'local')  63.3 us
    all_to_all x1, waiting for transfers between devices, body(): lax.all_to_all(outbound.astype(jnp.bfloat16), 'group', split_axis=0, conc...  58.9 us
    psum x1, blocking collectives, body(): lax.psum((grads[0][0], grads[0][1], grads[1][0], grads[1][1], grads[2][0]...  41.1 us
    scatter-add x1, other arithmetic, body(): jax.ops.segment_sum(returned, served_flat, num_segments=segment_count)  39.3 us
    all_to_all x1, waiting for transfers between devices, body(): lax.all_to_all(served_rows, 'group', split_axis=0, concat_axis=0, tiled=T...  38.3 us
    gather x1, local copies, waits for them, and re-layouts, body(): outgoing = keys_padded[source].reshape(groups, capacity)  34.5 us
    psum x1, waiting for transfers between devices, body(): inner = lax.psum(r_part, 'group')  33.6 us
  transfers between devices with their start and end apart: 9, of which 8 were waited for; matrix products, arithmetic and copies ran while one was open for 24% of the time, Pallas kernels for 0%

profile of v1, /device:TPU:0, one launch (start us, length us, event | category | flops | bytes accessed | tf_op | source)
XLA Modules:
  0.0 679.7 jit_solution(4859317630325263572)
XLA Ops:
  11.3 12.8 %scatter_custom_fusion = s32[6656]{0:T(1024)S(1)} fusion(s32[3328]{0:T(1024)S(1)} %fusion.38, s32[3328]{0:T(1024)S(1)} %iota.29, s32[]{:T(128)} %constant.27.clone.1), kind=kCustom, calls=%fused_computation.84 | custom fusion | bytes 26628 | tf_op jit(solution)/shard_map/scatter | solution.py:117
  24.1 34.5 %gather_fusion = s32[6656]{0:T(1024)S(1)} fusion(s32[3329]{0:T(1024)S(1)} %pad_add_fusion, s32[7168]{0:T(1024)S(1)} %pad_clamp_fusion.1), kind=kCustom, calls=%fused_computation | custom fusion | bytes 79872 | tf_op jit(solution)/shard_map/gather | solution.py:121
  59.3 7.3 %all-to-all-start = ((s32[8,1,832]{2,1,0:T(1,128)}), s32[8,1,832]{2,1,0:T(1,128)S(1)}, u32[]{:S(2)}, u32[]{:S(2)}) async-start(s32[8,1,832]{2,1,0:T(1,128)} %all_to_all.14), calls=%async_computation | async-start | bytes 57344 | tf_op jit(solution)/shard_map/all_to_all | solution.py:123
  66.6 2.5 copy.64
  69.3 4.0 all-to-all-done
  73.5 14.3 %gather_fusion.1 = bf16[6656,128]{1,0:T(8,128)(2,1)} fusion(bf16[3328,128]{1,0:T(8,128)(2,1)S(1)} %reshape.127, s32[7168]{0:T(1024)S(1)} %pad_clamp_fusion), kind=kCustom, calls=%fused_computation.1 | custom fusion | bytes 3434496 | tf_op jit(solution)/shard_map/gather | solution.py:124
  87.7 3.7 all-to-all-start.1
  91.8 38.3 %all-to-all-done.1 = bf16[8,832,128]{2,1,0:T(8,128)(2,1)S(1)} async-done(((bf16[8,832,128]{2,1,0:T(8,128)(2,1)}), bf16[8,832,128]{2,1,0:T(8,128)(2,1)S(1)}, u32[]{:S(2)}, u32[]{:S(2)}) %all-to-all-start.1) | async-done | bytes 1703968 | tf_op jit(solution)/shard_map/all_to_all | solution.py:125
  130.1 6.5 gather_fusion.2
  137.4 7.3 %fusion.5 = (bf16[128,26,128]{2,0,1:T(8,128)(2,1)S(1)}, f32[26,128,128]{2,1,0:T(8,128)}) fusion(f32[128,26,128]{2,1,0:T(8,128)S(1)} %reshape.131, f32[256,26,128]{2,0,1:T(8,128)} %all-gather.3.cloned.1.call-done, s32[128,26]{0,1:T(8,128)S(1)} %copy-done.25), kind=kOutput, calls=%fused_computation.19 | convolution fusion | flops 1310326784 | bytes 7681024 | tf_op jit(solution)/shard_map/btr,rtd->btd/dot_general | solution.py:132
  146.5 4.9 gather_fusion.3
  151.9 2.3 convolution_add_fusion.1
  159.2 19.0 %scatter_fusion = f32[128,27,27]{0,2,1:T(8,128)S(1)} fusion(f32[128,27,27]{0,2,1:T(8,128)S(1)} %broadcast_in_dim.21, s32[351]{0:T(512)S(1)} %copy-done, f32[351,128]{1,0:T(8,128)S(1)} %convolution_bitcast_fusion), kind=kCustom, calls=%fused_computation.6 | custom fusion | bytes 541944 | tf_op jit(solution)/shard_map/scatter | solution.py:33
  178.5 2.9 copy.87
  181.4 3.3 fusion.14
  184.7 6.2 fusion.4
  190.9 2.5 bitcast_multiply_fusion
  194.3 14.3 %gather_fusion.4 = bf16[6656,128]{1,0:T(8,128)(2,1)} fusion(bf16[3329,128]{1,0:T(8,128)(2,1)S(1)} %concatenate.24, s32[7168]{0:T(1024)S(1)} %pad_clamp_fusion.1), kind=kCustom, calls=%fused_computation.4 | custom fusion | bytes 3434496 | tf_op jit(solution)/shard_map/gather | solution.py:145
  208.6 3.6 all-to-all-start.2
  213.0 58.9 %all-to-all-done.2 = bf16[8,832,128]{2,1,0:T(8,128)(2,1)S(1)} async-done(((bf16[8,832,128]{2,1,0:T(8,128)(2,1)}), bf16[8,832,128]{2,1,0:T(8,128)(2,1)S(1)}, u32[]{:S(2)}, u32[]{:S(2)}) %all-to-all-start.2) | async-done | bytes 1703968 | tf_op jit(solution)/shard_map/all_to_all | solution.py:147
  271.9 39.3 %scatter_custom_fusion.2 = f32[3328,128]{1,0:T(8,128)S(1)} fusion(s32[6656]{0:T(1024)} %reshape.188, bf16[6656,128]{1,0:T(8,128)(2,1)S(1)} %bitcast.55, f32[]{:T(128)} %constant.24.clone.1), kind=kCustom, calls=%fused_computation.9 | custom fusion | flops 1703936 | bytes 3408384 | tf_op jit(solution)/shard_map/scatter-add | solution.py:154
  317.4 2.8 fusion.24
  320.3 33.6 %all-reduce.7.cloned.1.call-done = f32[256,26,128]{0,2,1:T(8,128)} async-done(((f32[256,26,128]{0,2,1:T(8,128)}), f32[256,26,128]{0,2,1:T(8,128)}) %all-reduce.7.cloned.1.call-update) | async-done | bytes 3407888 | tf_op jit(solution)/shard_map/psum | solution.py:169
  353.9 26.9 %reduce-scatter.2.cloned.1.call-done = bf16[32,26,128]{2,1,0:T(8,128)(2,1)} async-done(((bf16[128,26,128]{2,1,0:T(8,128)(2,1)}), bf16[32,26,128]{2,1,0:T(8,128)(2,1)}) %reduce-scatter.2.cloned.1.call-update) | async-done | bytes 213008 | tf_op jit(solution)/shard_map/reduce_scatter | solution.py:157
  384.4 41.1 %all-reduce.1 = (f32[1024]{0:T(1024)S(1)}, f32[1024]{0:T(1024)S(1)}, f32[512]{0:T(512)S(1)}, f32[256]{0:T(256)S(1)}) all-reduce(f32[1024]{0:T(1024)S(1)} %get-tuple-element.50, f32[1024]{0:T(1024)S(1)} %get-tuple-element.52, f32[512]{0:T(512)} %get-tuple-element.54, ...), channel_id=1, replica_groups=mesh['group'=8,'local'=4] {'group','local'}, use_global_device_ids=true, to_apply=%region_10.11 | all-reduce | flops 2816 | bytes 22528 | tf_op jit(solution)/shard_map/psum | solution.py:175
  428.7 143.8 %all-reduce.11.cloned.1.call-done = (f32[479,1024]{1,0:T(8,128)}, f32[1024,1024]{1,0:T(8,128)}, f32[1024,512]{1,0:T(8,128)}, f32[512,256]{1,0:T(8,128)}) async-done(((f32[479,1024]{1,0:T(8,128)}, f32[1024,1024]{1,0:T(8,128)}, f32[1024,512]{1,0:T(8,128)}, f32[512,256]{1,0:T(8,128)}), (f32[479,1024]{1,0:T(8,128)}, f32[1024,1024]{1,0:T(8,128)}, f32[1024,512]{1,0:T(8,128)}, ...) | async-done | bytes 8777744 | tf_op jit(solution)/shard_map/psum | solution.py:175
  572.5 2.1 multiply_subtract_fusion.4
  574.6 3.4 multiply_subtract_fusion.2
  581.4 2.7 multiply_subtract_fusion
  584.2 63.3 %all-reduce.9.cloned.1.call-done = f32[256,26,128]{0,2,1:T(8,128)} async-done(((f32[256,26,128]{0,2,1:T(8,128)}), f32[256,26,128]{0,2,1:T(8,128)}) %all-reduce.9.cloned.1.call-update) | async-done | bytes 3407888 | tf_op jit(solution)/shard_map/psum | solution.py:170
  650.8 19.2 %all-gather.5.cloned.1.call-done = f32[128,26,128]{2,0,1:T(8,128)} async-done(((f32[32,26,128]{2,0,1:T(8,128)}), f32[128,26,128]{2,0,1:T(8,128)}) %all-gather.5.cloned.1.call-update) | async-done | bytes 1703952 | tf_op jit(solution)/shard_map/all_gather | solution.py:162
  670.0 2.8 copy.113
  (137 shorter events, 35.1 us)
Async XLA Ops:
  7.2 129.7 %all-gather.3.cloned.1.call-start = ((), (), s32[]{:S(2)}) async-start(), calls=%async_computation.4 | async-start | bytes 4259840 | tf_op jit(solution)/shard_map/all_gather | solution.py:127
  59.3 14.0 %all-to-all-start = ((s32[8,1,832]{2,1,0:T(1,128)}), s32[8,1,832]{2,1,0:T(1,128)S(1)}, u32[]{:S(2)}, u32[]{:S(2)}) async-start(s32[8,1,832]{2,1,0:T(1,128)} %all_to_all.14), calls=%async_computation | async-start | bytes 57344 | tf_op jit(solution)/shard_map/all_to_all | solution.py:123
  69.1 18.6 %copy-start.3 = (f32[128,26,128]{2,1,0:T(8,128)}, f32[128,26,128]{2,1,0:T(8,128)S(1)}, u32[]{:S(2)}) copy-start(f32[128,26,128]{2,1,0:T(8,128)S(1)} %copy.64) | copy-start | bytes 5111812
  87.7 4.0 copy-start.22
  87.7 42.4 %all-to-all-start.1 = ((bf16[8,832,128]{2,1,0:T(8,128)(2,1)}), bf16[8,832,128]{2,1,0:T(8,128)(2,1)S(1)}, u32[]{:S(2)}, u32[]{:S(2)}) async-start(bf16[8,832,128]{2,1,0:T(8,128)(2,1)} %bitcast.54), calls=%async_computation.1 | async-start | bytes 3407872 | tf_op jit(solution)/shard_map/all_to_all | solution.py:125
  91.5 262.4 %all-reduce.7.cloned.1.call-start = ((), (), s32[]{:S(2)}) async-start(), calls=%async_computation.7 | async-start | bytes 6815744 | tf_op jit(solution)/shard_map/psum | solution.py:169
  136.9 7.8 %copy-start.1 = (f32[128,26,128]{2,1,0:T(8,128)}, f32[128,26,128]{2,1,0:T(8,128)S(1)}, u32[]{:S(2)}) copy-start(f32[128,26,128]{2,1,0:T(8,128)S(1)} %reshape.131) | copy-start | bytes 5111812
  144.7 6.7 copy-start.5
  144.8 6.7 copy-start.28
  145.4 6.4 copy-start.29
  151.8 4.8 copy-start.10
  151.8 2.3 copy-start.13
  151.8 2.3 copy-start.30
  156.1 2.6 copy-start.23
  158.7 19.5 %copy-start.20 = (bf16[128,1024]{1,0:T(8,128)(2,1)}, bf16[128,1024]{1,0:T(8,128)(2,1)S(1)}, u32[]{:S(2)}) copy-start(bf16[128,1024]{1,0:T(8,128)(2,1)S(1)} %get-tuple-element.51) | copy-start | bytes 786436
  181.4 3.4 copy-start.2
  208.6 63.3 %all-to-all-start.2 = ((bf16[8,832,128]{2,1,0:T(8,128)(2,1)}), bf16[8,832,128]{2,1,0:T(8,128)(2,1)S(1)}, u32[]{:S(2)}, u32[]{:S(2)}) async-start(bf16[8,832,128]{2,1,0:T(8,128)(2,1)} %bitcast.10), calls=%async_computation.2 | async-start | bytes 3407872 | tf_op jit(solution)/shard_map/all_to_all | solution.py:147
  212.2 168.6 %reduce-scatter.2.cloned.1.call-start = ((), (), s32[]{:S(2)}) async-start(), calls=%async_computation.5 | async-start | bytes 1310720 | tf_op jit(solution)/shard_map/reduce_scatter | solution.py:157
  311.3 2.7 copy-start.21
  312.5 3.1 copy-start.16
  312.5 3.1 copy-start.24
  312.5 260.0 %all-reduce.11.cloned.1.call-start = ((), (), s32[]{:S(2)}) async-start(), calls=%async_computation.9 | async-start | bytes 17563648 | tf_op jit(solution)/shard_map/psum | solution.py:175
  313.9 3.5 copy-start.11
  313.9 3.5 copy-start.19
  320.2 327.3 %all-reduce.9.cloned.1.call-start = ((), (), s32[]{:S(2)}) async-start(), calls=%async_computation.8 | async-start | bytes 6815744 | tf_op jit(solution)/shard_map/psum | solution.py:170
  353.8 29.2 %copy-start.7 = (f32[64,26,128]{2,0,1:T(8,128)S(1)}, f32[64,26,128]{2,0,1:T(8,128)}, u32[]{:S(2)}) copy-start(f32[64,26,128]{2,0,1:T(8,128)} %param.25) | copy-start | bytes 2555908
  353.9 316.1 %all-gather.5.cloned.1.call-start = ((), (), s32[]{:S(2)}) async-start(), calls=%async_computation.6 | async-start | bytes 2129920 | tf_op jit(solution)/shard_map/all_gather | solution.py:162
  383.0 191.5 %copy-start.6 = (bf16[479,1024]{1,0:T(8,128)(2,1)S(1)}, bf16[479,1024]{1,0:T(8,128)(2,1)}, u32[]{:S(2)}) copy-start(bf16[479,1024]{1,0:T(8,128)(2,1)} %param.29) | copy-start | bytes 2942980
  572.5 5.5 copy-start.14
  574.6 3.4 copy-start.12
  574.6 5.1 copy-start.9
  578.0 3.4 copy-start.4
  (10 other events, 15.1 us)
Sparse Core Ops, SparseCore 0:
  9.5 32.7 all-gather.2
  191.1 162.7 all-reduce.6
  356.9 23.8 reduce-scatter.1
  387.5 184.9 all-reduce.10
  574.7 72.7 all-reduce.8
  649.5 20.4 all-gather.4
